TPU v7x, 32 devices: a whole 2x2x4 slice. The times are simulated.
32 devices in a mesh: prow: 4 (over y, x), pcol: 8 (over z, core).
Axes of the slice: x: 2, y: 2, z: 4, core: 2. Of those that a mesh axis runs over, the one named last changes fastest.
Arguments:
- covariance: float32 [16384, 16384], P(('prow', 'pcol')), may hold values from -600 to 600, as said below
- factor_left: float32 [64, 16384], P(None, ('prow', 'pcol')), may hold values from -6 to 6
- factor_right: float32 [64, 16384], P('prow', 'pcol'), may hold values from -3 to 3
Outputs:
- whitened: float32 [16384, 16384], P('prow', 'pcol')
Inputs may be any that keep to these rules, and one draw needn't show every extreme that they name: `covariance`: entries are real-valued and of full rank.
All inputs are finite; a program needn't handle non-finite values.
Results may differ from a plain program's by a relative error of at most 0.00007.
Values sent between devices are 32-bit elements; how exact they have to be, the bound alone decides.
A program may use at most 192 MiB of HBM per device.

v0:
```python
import functools

import jax
import jax.numpy as jnp
from jax import lax
from jax.experimental import pallas as pl
from jax.experimental.pallas import tpu as pltpu
from jax.sharding import PartitionSpec as P

ORDER = 16384
TILE = 64


epsilon = 1e-06


def deal_columns(source):
    height = source.shape[0]
    breadth = source.shape[1]
    grid_cols = lax.axis_size("pcol")
    arranged = (
        source.reshape(height, breadth // (TILE * grid_cols), grid_cols, TILE)
        .transpose(0, 2, 1, 3)
        .reshape(height, breadth)
    )
    return lax.all_to_all(arranged, "pcol", split_axis=1, concat_axis=0, tiled=True)


def order_rows(source):
    height = source.shape[0]
    breadth = source.shape[1]
    grid_rows = lax.axis_size("prow")
    grouped = source.reshape(height // (TILE * grid_rows), grid_rows, TILE, breadth)
    return grouped.transpose(1, 0, 2, 3).reshape(height, breadth)


def body(covariance, factor_left, factor_right):
    right_panel = lax.all_gather(factor_right, "prow", axis=0, tiled=True)
    dealt = deal_columns(covariance)
    left_block = lax.all_gather(factor_left, "pcol", axis=1, tiled=True).T
    tiles_moved, left_rows = (
        lax.all_to_all(order_rows(dealt), "prow", split_axis=0, concat_axis=0, tiled=True),
        lax.all_to_all(order_rows(left_block), "prow", split_axis=0, concat_axis=0, tiled=True),
    )
    corrected = tiles_moved + jnp.dot(
        left_rows, right_panel, precision=lax.Precision.HIGHEST, preferred_element_type=jnp.float32
    )
    squared = corrected * corrected
    row_total = lax.psum(jnp.sum(squared, axis=1), "pcol")
    col_total = lax.psum(jnp.sum(squared, axis=0), "prow")
    row_mean = row_total / ORDER + epsilon
    col_mean = col_total / ORDER + epsilon
    return corrected * lax.rsqrt(jnp.sqrt(row_mean[:, None] * col_mean[None, :]))


def flip(index, size, bits):
    out, unit = 0, 1
    while unit < size:
        out = out + unit * ((index // unit + bits // unit) % 2)
        unit *= 2
    return out


def deal_kernel(grid_cols, src, dst):
    rows = src.shape[0]
    low = lax.broadcasted_iota(jnp.int32, (rows, 2 * TILE), 1) < TILE
    lanes = 2 * TILE
    for pair in range(grid_cols // 2):
        for m in range(src.shape[1] // (lanes * grid_cols)):
            at = (pair + grid_cols * m) * lanes
            first = src[:, at:at + lanes]
            at += grid_cols // 2 * lanes
            second = src[:, at:at + lanes]
            dst[0, 2 * pair, :, m * lanes:(m + 1) * lanes] = jnp.where(low, first, pltpu.roll(second, TILE, 1))
            dst[0, 2 * pair + 1, :, m * lanes:(m + 1) * lanes] = jnp.where(low, pltpu.roll(first, TILE, 1), second)


def deal(covariance, grid_rows, grid_cols):
    height, breadth = covariance.shape
    tiles = height // TILE
    step = TILE // 2
    return pl.pallas_call(
        functools.partial(deal_kernel, grid_cols),
        grid=(tiles, TILE // step),
        in_specs=[pl.BlockSpec((step, breadth), lambda j, h: (j * (TILE // step) + h, 0))],
        out_specs=pl.BlockSpec(
            (1, grid_cols, step, breadth // grid_cols),
            lambda j, h: (j % grid_rows, 0, (j // grid_rows) * (TILE // step) + h, 0),
        ),
        out_shape=jax.ShapeDtypeStruct(
            (grid_rows, grid_cols, height // grid_rows, breadth // grid_cols), jnp.float32
        ),
        compiler_params=pltpu.CompilerParams(vmem_limit_bytes=40 * 1024 * 1024),
    )(covariance)


def exchange_kernel(
    grid_rows, grid_cols, tiles, left, right, got, got_left, got_right,
    tile_send, tile_recv, left_send, left_recv, right_send, right_recv, swap_send, swap_recv, own,
):
    chips = grid_cols // 2
    p = lax.axis_index("prow")
    q = lax.axis_index("pcol")
    z, core = q // 2, q % 2
    height = tiles.shape[2]

    def target(dp, dz, dc):
        to_p = flip(p, grid_rows, dp)
        to_q = 2 * flip(z, chips, dz) + (core + dc) % 2
        return to_p, to_q

    def offsets(distances):
        return [
            (dp, dz, dc)
            for dp in range(grid_rows)
            for dz in distances
            for dc in range(2)
            if (dp, dz, dc) != (0, 0, 0)
        ]

    across = offsets(range(chips - 1, chips // 2 - 1, -1))
    within = offsets(range(chips // 2 - 1, -1, -1))
    beside = (z + z // 2) % 2
    everyone = [
        tuple(beside * a + (1 - beside) * b for a, b in zip(first, second))
        for first, second in zip(across + within, within + across)
    ]
    barrier = pltpu.get_barrier_semaphore()
    for offset in everyone:
        pl.semaphore_signal(barrier, inc=1, device_id=target(*offset), device_id_type=pl.DeviceIdType.MESH)
    pl.semaphore_wait(barrier, len(everyone))

    def copy(src, dst, send, recv, to):
        return pltpu.make_async_remote_copy(
            src_ref=src, dst_ref=dst, send_sem=send, recv_sem=recv,
            device_id=to, device_id_type=pl.DeviceIdType.MESH,
        )

    my_slot = p * grid_cols + q
    started = []
    kept = [
        pltpu.make_async_copy(left.at[p], got_left.at[core, p * chips + z], own.at[0]),
        pltpu.make_async_copy(right, got_right.at[p], own.at[1]),
    ]
    for one in kept:
        one.start()
    lefts = []
    for dz in range(chips):
        for dp in range(grid_rows):
            if (dp, dz) != (0, 0):
                n = dz * grid_rows + dp
                to = target(dp, dz, 0)
                one = copy(left.at[to[0]], got_left.at[core, p * chips + z], left_send.at[n], left_recv.at[n], to)
                one.start()
                lefts.append(one)
    for dp in range(1, grid_rows):
        one = copy(right, got_right.at[p], right_send.at[dp], right_recv.at[dp], target(dp, 0, 0))
        one.start()
        started.append(one)
    for n, offset in enumerate(everyone):
        to = target(*offset)
        slot = (offset[0] * chips + offset[1]) * 2 + offset[2]
        one = copy(
            tiles.at[to[0], to[1]], got.at[pl.ds(pl.multiple_of(my_slot * height, height), height)],
            tile_send.at[n], tile_recv.at[slot], to,
        )
        one.start()
        started.append(one)
    for one in kept:
        one.wait()
    for one in lefts:
        one.wait()
    swap = copy(got_left.at[core], got_left.at[core], swap_send, swap_recv, target(0, 0, 1))
    swap.start()

    piece = TILE // 2

    def keep(scratch, sem_in, sem_out):
        for n in range(height // piece):
            one = pltpu.make_async_copy(tiles.at[p, q, pl.ds(n * piece, piece)], scratch.at[n], sem_in.at[n])
            one.start()
        for n in range(height // piece):
            pltpu.make_async_copy(tiles.at[p, q, pl.ds(n * piece, piece)], scratch.at[n], sem_in.at[n]).wait()
            pltpu.make_async_copy(
                scratch.at[n], got.at[pl.ds(pl.multiple_of(my_slot * height + n * piece, piece), piece)], sem_out.at[n]
            ).start()
        for n in range(height // piece):
            pltpu.make_async_copy(
                scratch.at[n], got.at[pl.ds(pl.multiple_of(my_slot * height + n * piece, piece), piece)], sem_out.at[n]
            ).wait()

    pl.run_scoped(
        keep,
        pltpu.VMEM((height // piece, piece, tiles.shape[3]), jnp.float32),
        pltpu.SemaphoreType.DMA((height // piece,)),
        pltpu.SemaphoreType.DMA((height // piece,)),
    )
    swap.wait()
    for one in started:
        one.wait()


def exchange(tiles, left, right):
    grid_rows, grid_cols, height, breadth = tiles.shape
    everyone = grid_rows * grid_cols
    dma = pltpu.SemaphoreType.DMA
    anywhere = pl.BlockSpec(memory_space=pl.ANY)
    return pl.pallas_call(
        functools.partial(exchange_kernel, grid_rows, grid_cols),
        out_shape=(
            jax.ShapeDtypeStruct((everyone * height, breadth), jnp.float32),
            jax.ShapeDtypeStruct((2, everyone // 2) + left.shape[1:], jnp.float32),
            jax.ShapeDtypeStruct((grid_rows,) + right.shape, jnp.float32),
        ),
        in_specs=[anywhere] * 3,
        out_specs=(anywhere,) * 3,
        scratch_shapes=[
            dma((everyone,)), dma((everyone,)), dma((everyone // 2,)), dma((everyone // 2,)),
            dma((grid_rows,)), dma((grid_rows,)), dma, dma, dma((2,)),
        ],
        compiler_params=pltpu.CompilerParams(collective_id=0, has_side_effects=True),
    )(tiles, left, right)


def direct_body(covariance, factor_left, factor_right):
    grid_rows, grid_cols = lax.axis_size("prow"), lax.axis_size("pcol")
    rank, height = factor_left.shape
    each = height // grid_rows
    tiles = deal(covariance, grid_rows, grid_cols)
    left = (
        factor_left.reshape(rank, each // TILE, grid_rows, TILE).transpose(2, 0, 1, 3).reshape(grid_rows, rank, each)
    )
    moved, lefts, rights = exchange(tiles, left, factor_right)
    chips = grid_cols // 2
    left_rows = (
        lefts.reshape(2, grid_rows, chips, rank, each).transpose(1, 2, 0, 4, 3).reshape(-1, rank)
    )
    right_panel = rights.reshape(rank, -1)
    corrected = moved + jnp.dot(
        left_rows, right_panel, precision=lax.Precision.HIGH, preferred_element_type=jnp.float32
    )
    squared = corrected * corrected
    row_total = lax.psum(jnp.sum(squared, axis=1), "pcol")
    col_total = lax.psum(jnp.sum(squared, axis=0), "prow")
    row_mean = row_total / ORDER + epsilon
    col_mean = col_total / ORDER + epsilon
    return corrected * lax.rsqrt(jnp.sqrt(row_mean[:, None] * col_mean[None, :]))


def power_of_two(n):
    return n & (n - 1) == 0


def chosen(mesh, covariance):
    grid_rows, grid_cols = mesh.shape["prow"], mesh.shape["pcol"]
    tiles = covariance.shape[0] // (grid_rows * grid_cols * TILE)
    fits = tiles > 0 and tiles % grid_rows == 0 and (tiles // grid_rows) % 2 == 0
    across = covariance.shape[1] // (TILE * grid_cols)
    fits = fits and power_of_two(grid_rows) and power_of_two(grid_cols) and grid_cols > 1 and across % 2 == 0
    return direct_body if fits else body


def solution(mesh):
    placed = (P(("prow", "pcol"), None), P(None, ("prow", "pcol")), P("prow", "pcol"))

    def run(covariance, factor_left, factor_right):
        return jax.shard_map(
            chosen(mesh, covariance), mesh=mesh, in_specs=placed, out_specs=P("prow", "pcol"), check_vma=False
        )(covariance, factor_left, factor_right)

    return run
```

profile of v0, /device:TPU:0, one launch (start us, length us, event | category | flops | bytes accessed | tf_op | source)
XLA Modules:
  0.0 870.7 jit_solution(7856806918280430099)
XLA Ops:
  0.0 1.1 reshape.17
  1.1 0.1 copy.10
  1.2 0.8 reshape.18.left
  2.0 30.4 %shard_map.37.tiles = f32[4,8,128,2048]{3,2,1,0:T(8,128)} custom-call(f32[512,16384]{1,0:T(8,128)} %src.1), custom_call_target="tpu_custom_call" | custom-call | tf_op jit(solution)/shard_map/pallas_call | solution.py:82
  32.4 741.0 %shard_map.38 = (f32[4096,2048]{1,0:T(8,128)}, f32[2,16,64,128]{3,2,1,0:T(8,128)}, f32[4,16,2048]{2,1,0:T(8,128)}) custom-call(f32[4,8,128,2048]{3,2,1,0:T(8,128)} %shard_map.37.tiles, f32[4,64,128]{2,1,0:T(8,128)} %reshape.18.left, f32[16,2048]{1,0:T(8,128)} %right.1), custom_call_target="tpu_custom_call" | custom-call | tf_op jit(solution)/shard_map/pallas_call | solution.py:208
  773.4 2.0 copy.9
  775.4 0.8 reshape.20
  776.3 28.8 %multiply_reduce_fusion.1 = (f32[4096]{0:T(1024)S(1)}, f32[2048]{0:T(1024)S(1)}, f32[4096,2048]{1,0:T(8,128)}) fusion(f32[4096,2048]{1,0:T(8,128)} %get-tuple-element.8, f32[4096,64]{0,1:T(8,128)S(1)} %reshape.20, f32[64,2048]{1,0:T(8,128)} %bitcast.15), kind=kOutput, calls=%fused_computation.2 | convolution fusion | flops 3254773760 | bytes 68706304 | tf_op jit(solution)/shard_map/dot_general | solution.py:239
  805.1 28.4 %psum.14 = f32[4096]{0:T(1024)S(1)} all-reduce(f32[4096]{0:T(1024)S(1)} %get-tuple-element.11), channel_id=1, replica_groups=mesh['prow'=4,'pcol'=8] {'pcol'}, use_global_device_ids=true, to_apply=%region_1.0 | all-reduce | flops 4096 | bytes 32768 | tf_op jit(solution)/shard_map/psum | solution.py:243
  833.4 10.1 %psum.15 = f32[2048]{0:T(1024)S(1)} all-reduce(f32[2048]{0:T(1024)S(1)} %get-tuple-element.12), channel_id=1, replica_groups=mesh['prow'=4,'pcol'=8] {'prow'}, use_global_device_ids=true, to_apply=%region_3.0 | all-reduce | flops 2048 | bytes 16384 | tf_op jit(solution)/shard_map/psum | solution.py:244
  843.6 27.1 %rsqrt_multiply_fusion = f32[4096,2048]{1,0:T(8,128)} fusion(f32[4096,2048]{1,0:T(8,128)} %get-tuple-element.13, f32[2048]{0:T(1024)S(1)} %multiply_add_fusion.1, f32[4096]{0:T(1024)S(1)} %multiply_add_fusion), kind=kLoop, calls=%fused_computation | loop fusion | flops 16777216 | bytes 67133440 | tf_op jit(solution)/shard_map/mul | solution.py:247
  (2 shorter events, 0.0 us)
where the time goes:
time: 871 us
  Pallas kernels  771 us (89%)
  blocking collectives  38.5 us (4%)
  matrix products  28.8 us (3%)
  other arithmetic  27.1 us (3%)
    pallas_call x1, Pallas kernels, exchange(): pl.pallas_call(functools.partial(exchange_kernel, grid_rows, grid_cols),...  741 us
    pallas_call x1, Pallas kernels, deal(): pl.pallas_call(functools.partial(deal_kernel, grid_cols), grid=(tiles, TI...  30.4 us
    dot_general x1, matrix products, direct_body(): jnp.dot(left_rows, right_panel, precision=lax.Precision.HIGH, preferred_e...  28.8 us
    psum x1, blocking collectives, direct_body(): row_total = lax.psum(jnp.sum(squared, axis=1), 'pcol')  28.4 us
    mul x1, other arithmetic, direct_body(): corrected * lax.rsqrt(jnp.sqrt(row_mean[:, None] * col_mean[None, :]))  27.1 us

commit v1 on v0

v1 whole, which is shorter than its diff:
```python
import functools

import jax
import jax.numpy as jnp
from jax import lax
from jax.experimental import pallas as pl
from jax.experimental.pallas import tpu as pltpu
from jax.sharding import PartitionSpec as P

ORDER = 16384
TILE = 64


epsilon = 1e-06


def deal_columns(source):
    height = source.shape[0]
    breadth = source.shape[1]
    grid_cols = lax.axis_size("pcol")
    arranged = (
        source.reshape(height, breadth // (TILE * grid_cols), grid_cols, TILE)
        .transpose(0, 2, 1, 3)
        .reshape(height, breadth)
    )
    return lax.all_to_all(arranged, "pcol", split_axis=1, concat_axis=0, tiled=True)


def order_rows(source):
    height = source.shape[0]
    breadth = source.shape[1]
    grid_rows = lax.axis_size("prow")
    grouped = source.reshape(height // (TILE * grid_rows), grid_rows, TILE, breadth)
    return grouped.transpose(1, 0, 2, 3).reshape(height, breadth)


def body(covariance, factor_left, factor_right):
    right_panel = lax.all_gather(factor_right, "prow", axis=0, tiled=True)
    dealt = deal_columns(covariance)
    left_block = lax.all_gather(factor_left, "pcol", axis=1, tiled=True).T
    tiles_moved, left_rows = (
        lax.all_to_all(order_rows(dealt), "prow", split_axis=0, concat_axis=0, tiled=True),
        lax.all_to_all(order_rows(left_block), "prow", split_axis=0, concat_axis=0, tiled=True),
    )
    corrected = tiles_moved + jnp.dot(
        left_rows, right_panel, precision=lax.Precision.HIGHEST, preferred_element_type=jnp.float32
    )
    squared = corrected * corrected
    row_total = lax.psum(jnp.sum(squared, axis=1), "pcol")
    col_total = lax.psum(jnp.sum(squared, axis=0), "prow")
    row_mean = row_total / ORDER + epsilon
    col_mean = col_total / ORDER + epsilon
    return corrected * lax.rsqrt(jnp.sqrt(row_mean[:, None] * col_mean[None, :]))


def flip(index, size, bits):
    out, unit = 0, 1
    while unit < size:
        out = out + unit * ((index // unit + bits // unit) % 2)
        unit *= 2
    return out


SLAB = TILE // 2
LANES = 128
CHUNK = 256
STAGES = 4


def deal_slab(grid_cols, src, dst):
    low = lax.broadcasted_iota(jnp.int32, (src.shape[0], LANES), 1) < TILE
    for pair in range(grid_cols // 2):
        for m in range(src.shape[1] // (LANES * grid_cols)):
            at = (pair + grid_cols * m) * LANES
            first = src[:, at:at + LANES]
            at += grid_cols // 2 * LANES
            second = src[:, at:at + LANES]
            dst[2 * pair, :, m * LANES:(m + 1) * LANES] = jnp.where(low, first, pltpu.roll(second, TILE, 1))
            dst[2 * pair + 1, :, m * LANES:(m + 1) * LANES] = jnp.where(low, pltpu.roll(first, TILE, 1), second)


def exchange_kernel(
    grid_rows, grid_cols,
    cov, left, right, got, row_parts, col_parts, tiles,
    slab_in, slab_out, left_own, lefts, rights, right_split, col_sum,
    in_sem, out_sem, tile_send, tile_recv, plane_send, plane_recv, block_send, block_recv,
    relay_send, relay_recv, swap_send, swap_recv, right_send, right_recv, own_sem,
    row_send, row_recv, col_send, col_recv,
):
    chips = grid_cols // 2
    p, q = lax.axis_index("prow"), lax.axis_index("pcol")
    z, core = q // 2, q % 2
    height = tiles.shape[2]
    rank = left.shape[0]
    beside = (z + z // 2) % 2
    half = z // 2
    mate = flip(z, chips, 1)
    far = jnp.maximum(z, 3 - z)

    def copy(src, dst, send, recv, to):
        return pltpu.make_async_remote_copy(
            src_ref=src, dst_ref=dst, send_sem=send, recv_sem=recv,
            device_id=to, device_id_type=pl.DeviceIdType.MESH,
        )

    def target(dp, dz, dc):
        return flip(p, grid_rows, dp), 2 * flip(z, chips, dz) + (core + dc) % 2

    barrier = pltpu.get_barrier_semaphore()
    for dp in range(grid_rows):
        for dz in range(chips):
            for dc in range(2):
                if (dp, dz, dc) != (0, 0, 0):
                    pl.semaphore_signal(
                        barrier, inc=1, device_id=target(dp, dz, dc), device_id_type=pl.DeviceIdType.MESH
                    )

    def slab_load(t, h):
        at = ((t % 2) * grid_rows + flip(p, grid_rows, t // 2)) * TILE + h * SLAB
        return pltpu.make_async_copy(cov.at[pl.ds(pl.multiple_of(at, SLAB), SLAB)], slab_in.at[h], in_sem.at[h])

    def slab_store(t, h):
        at = (t % 2) * TILE + h * SLAB
        return pltpu.make_async_copy(
            slab_out.at[t % 2, h],
            tiles.at[flip(p, grid_rows, t // 2), :, pl.ds(pl.multiple_of(at, SLAB), SLAB)],
            out_sem.at[t % 2, h],
        )

    for h in range(2):
        slab_load(0, h).start()

    low = lax.broadcasted_iota(jnp.int32, (rank, LANES), 1) < TILE
    for to in range(grid_rows):
        at = to // 2 * LANES
        first = left[:, at:at + LANES]
        at += grid_rows * TILE
        second = left[:, at:at + LANES]
        if to % 2 == 0:
            left_own[to] = jnp.where(low, first, pltpu.roll(second, TILE, 1))
        else:
            left_own[to] = jnp.where(low, pltpu.roll(first, TILE, 1), second)

    def plane(dp):
        return copy(
            left_own.at[flip(p, grid_rows, dp)], lefts.at[core, z, p],
            plane_send.at[dp], plane_recv.at[dp], target(dp, 0, 0),
        )

    def beside_right(dp):
        return copy(right, rights.at[p], right_send.at[dp], right_recv.at[dp], target(dp, 0, 0))

    keep_left = pltpu.make_async_copy(left_own.at[p], lefts.at[core, z, p], own_sem.at[0])
    keep_right = pltpu.make_async_copy(right, rights.at[p], own_sem.at[1])

    block = lefts.at[core, z]
    gate = 2 - half
    to_mate = copy(block, block, block_send.at[0], block_recv.at[z], (p, 2 * mate + core))
    to_gate = copy(block, block, block_send.at[1], block_recv.at[z], (p, 2 * gate + core))
    other = lefts.at[core, pl.ds(2 * (1 - half), 2)]
    relay = copy(other, other, relay_send, relay_recv, (p, 2 * mate + core))
    swap = copy(lefts.at[core], lefts.at[core], swap_send, swap_recv, target(0, 0, 1))
    own_rows = pl.ds(pl.multiple_of((p * grid_cols + q) * height, height), height)
    keep_tiles = pltpu.make_async_copy(tiles.at[p, q], got.at[own_rows], own_sem.at[2])

    def tile(dp, dz, dc, k):
        to = target(dp, dz, dc)
        at = (p * grid_cols + q) * height + k * TILE
        n = ((dp * chips + dz) * 2 + dc) * 2 + k
        return copy(
            tiles.at[to[0], to[1], pl.ds(pl.multiple_of(k * TILE, TILE), TILE)],
            got.at[pl.ds(pl.multiple_of(at, TILE), TILE)], tile_send.at[n], tile_recv.at[n], to,
        )

    def send_tiles(t, kind):
        dp, k = t // 2, t % 2
        for i in range(2):
            dz = kind * (3 - i) + (1 - kind) * (1 - i)
            for dc in range(2):
                mine = (dp + dz + dc) == 0

                @pl.when(jnp.logical_not(mine))
                def _():
                    tile(dp, dz, dc, k).start()

    def deal(t, carry):
        @pl.when(t < 2 * grid_rows)
        def _():
            for h in range(2):
                slab_load(t, h).wait()
                deal_slab(grid_cols, slab_in.at[h], slab_out.at[t % 2, h])

                @pl.when(t + 1 < 2 * grid_rows)
                def _():
                    slab_load(t + 1, h).start()

                slab_store(t, h).start()

                @pl.when((t == 0) & (h == 0))
                def _():
                    pl.semaphore_wait(barrier, grid_rows * grid_cols - 1)
                    keep_left.start()
                    for dp in range(1, grid_rows):
                        plane(dp).start()
                    keep_right.start()
                    for dp in range(1, grid_rows):
                        beside_right(dp).start()

        @pl.when(t == 0)
        def _():
            keep_left.wait()
            for dp in range(1, grid_rows):
                plane(dp).wait()
            to_gate.start()
            to_mate.start()

        @pl.when(t != 1)
        def _():
            s = jnp.maximum(t - 1, 0)
            for h in range(2):
                slab_store(s, h).wait()
            send_tiles(s, beside)

        return carry

    lax.fori_loop(0, 2 * grid_rows + 1, deal, 0)
    keep_tiles.start()

    to_gate.wait_send()
    to_mate.wait_send()

    def arrived(which):
        there = lefts.at[core, which]
        return copy(there, there, block_send.at[0], block_recv.at[which], (p, 2 * mate + core))

    arrived(mate).wait_recv()

    @pl.when(beside == 1)
    def _():
        for i in range(2):
            arrived(2 * (1 - half) + i).wait_recv()
        relay.start()

    def send_rest(t, carry):
        send_tiles(t, 1 - beside)
        return carry

    lax.fori_loop(0, 2 * grid_rows, send_rest, 0)

    keep_right.wait()
    for dp in range(1, grid_rows):
        beside_right(dp).wait()
    depth = right.shape[0]
    for n in range(grid_rows):
        value = rights[n]
        high = value.astype(jnp.bfloat16)
        rest = (value - high.astype(jnp.float32)).astype(jnp.bfloat16)
        right_split[n * depth:(n + 1) * depth] = high
        right_split[rank + n * depth:rank + (n + 1) * depth] = rest
        right_split[2 * rank + n * depth:2 * rank + (n + 1) * depth] = high
        right_split[3 * rank + n * depth:3 * rank + (n + 1) * depth] = jnp.zeros_like(high)
    col_sum[...] = jnp.zeros_like(col_sum)

    @pl.when(beside == 0)
    def _():
        relay.wait_recv()

    @pl.when(beside == 1)
    def _():
        relay.wait_send()

    swap.start()
    swap.wait()
    keep_tiles.wait()

    width = got.shape[1]

    def settle(m, carry):
        group = m // (2 * grid_rows)
        dz = jnp.where(group == 3, far, jnp.where(group == 2, 5 - far, group))
        dp, dc = m % (2 * grid_rows) // 2, m % 2
        from_p, from_q = target(dp, dz, dc)
        slot = from_p * grid_cols + from_q

        @pl.when(dp + dz + dc != 0)
        def _():
            for k in range(2):
                n = ((dp * chips + dz) * 2 + dc) * 2 + k
                there = got.at[pl.ds(pl.multiple_of(slot * height + k * TILE, TILE), TILE)]
                copy(
                    tiles.at[0, 0, pl.ds(0, TILE)], there, tile_send.at[n], tile_recv.at[n], (from_p, from_q)
                ).wait_recv()

        value = lefts[from_q % 2, from_q // 2, from_p]
        high = value.astype(jnp.bfloat16).astype(jnp.float32)
        stack = jnp.concatenate([high, high, value - high, jnp.zeros_like(high)], axis=0)
        factor = stack.T.astype(jnp.bfloat16)
        rows = pl.ds(pl.multiple_of(slot * height, height), height)
        total = jnp.zeros((height, LANES), jnp.float32)
        for at in range(0, width, CHUNK):
            here = slice(at, at + CHUNK)
            fixed = got[rows, here] + jnp.dot(
                factor, right_split[:, here], preferred_element_type=jnp.float32
            )
            got[rows, here] = fixed
            square = fixed * fixed
            for lane in range(0, CHUNK, LANES):
                total = total + square[:, lane:lane + LANES]
            part = square[0:8]
            for n in range(8, height, 8):
                part = part + square[n:n + 8]
            col_sum[:, here] += part
        row_parts[q, pl.ds(slot, 1)] = jnp.sum(total.T, axis=0, keepdims=True)
        return carry

    lax.fori_loop(0, grid_rows * grid_cols, settle, 0)
    col_parts[p] = jnp.sum(col_sum[...], axis=0, keepdims=True)

    def row_part(n):
        dz, dc = n // 2, n % 2
        return copy(row_parts.at[q], row_parts.at[q], row_send.at[n], row_recv.at[n], target(0, dz, dc))

    def col_part(dp):
        return copy(col_parts.at[p], col_parts.at[p], col_send.at[dp], col_recv.at[dp], target(dp, 0, 0))

    for n in range(grid_cols - 1, 0, -1):
        row_part(n).start()
    for dp in range(1, grid_rows):
        col_part(dp).start()

    def drain(n, carry):
        @pl.when(n > 1)
        def _():
            tile(n // (4 * chips), n // 4 % chips, n // 2 % 2, n % 2).wait_send()

        return carry

    lax.fori_loop(0, 2 * grid_rows * grid_cols, drain, 0)
    for n in range(1, grid_cols):
        row_part(n).wait()
    for dp in range(1, grid_rows):
        col_part(dp).wait()


def exchange(covariance, left, right):
    grid_rows, grid_cols = lax.axis_size("prow"), lax.axis_size("pcol")
    everyone = grid_rows * grid_cols
    rows, breadth = covariance.shape
    rank = left.shape[0]
    height, width = rows // grid_rows, breadth // grid_cols
    dma = pltpu.SemaphoreType.DMA
    vmem = pl.BlockSpec(memory_space=pltpu.VMEM)
    hbm = pl.BlockSpec(memory_space=pltpu.HBM)
    return pl.pallas_call(
        functools.partial(exchange_kernel, grid_rows, grid_cols),
        out_shape=(
            pltpu.VMEM((everyone * height, width), jnp.float32),
            pltpu.VMEM((grid_cols, everyone, height), jnp.float32),
            pltpu.VMEM((grid_rows, 1, width), jnp.float32),
            pltpu.HBM((grid_rows, grid_cols, height, width), jnp.float32),
        ),
        in_specs=[hbm, vmem, vmem],
        out_specs=(vmem, vmem, vmem, hbm),
        scratch_shapes=[
            pltpu.VMEM((2, SLAB, breadth), jnp.float32),
            pltpu.VMEM((2, 2, grid_cols, SLAB, width), jnp.float32),
            pltpu.VMEM((grid_rows, rank, height), jnp.float32),
            pltpu.VMEM((2, grid_cols // 2, grid_rows, rank, height), jnp.float32),
            pltpu.VMEM((grid_rows,) + right.shape, jnp.float32),
            pltpu.VMEM((4 * rank, width), jnp.bfloat16),
            pltpu.VMEM((8, width), jnp.float32),
            dma((2,)), dma((2, 2)), dma((2 * everyone,)), dma((2 * everyone,)),
            dma((grid_rows,)), dma((grid_rows,)), dma((2,)), dma((grid_cols // 2,)),
            dma, dma, dma, dma, dma((grid_rows,)), dma((grid_rows,)), dma((3,)),
            dma((grid_cols,)), dma((grid_cols,)), dma((grid_rows,)), dma((grid_rows,)),
        ],
        compiler_params=pltpu.CompilerParams(
            collective_id=0, has_side_effects=True, vmem_limit_bytes=22 * 1024 * 1024
        ),
    )(covariance, left, right)


def scale_kernel(order, got, row_parts, col_parts, out, stage, row_scale, sem):
    grid_cols, everyone, height = row_parts.shape
    width = got.shape[1]
    rows, cols = row_parts[0], col_parts[0]
    for n in range(1, grid_cols):
        rows = rows + row_parts[n]
    for n in range(1, col_parts.shape[0]):
        cols = cols + col_parts[n]
    row_scale[...] = lax.rsqrt(jnp.sqrt(rows / order + epsilon))
    col_scale = lax.rsqrt(jnp.sqrt(cols / order + epsilon))

    def store(n):
        return pltpu.make_async_copy(
            stage.at[n % STAGES], out.at[pl.ds(pl.multiple_of(n * height, height), height)], sem.at[n % STAGES]
        )

    def step(n, carry):
        @pl.when(n >= STAGES)
        def _():
            store(n - STAGES).wait()

        scale = jnp.broadcast_to(row_scale[pl.ds(n, 1)], (height, height)).T
        here = pl.ds(pl.multiple_of(n * height, height), height)
        for at in range(0, width, LANES):
            stage[n % STAGES, :, at:at + LANES] = got[here, at:at + LANES] * scale * col_scale[:, at:at + LANES]
        store(n).start()
        return carry

    lax.fori_loop(0, everyone, step, 0)
    for n in range(everyone - STAGES, everyone):
        store(n).wait()


def scaled(order, got, row_parts, col_parts):
    height, width = row_parts.shape[2], got.shape[1]
    vmem = pl.BlockSpec(memory_space=pltpu.VMEM)
    return pl.pallas_call(
        functools.partial(scale_kernel, order),
        out_shape=jax.ShapeDtypeStruct(got.shape, jnp.float32),
        in_specs=[vmem] * 3,
        out_specs=pl.BlockSpec(memory_space=pl.ANY),
        scratch_shapes=[
            pltpu.VMEM((STAGES, height, width), jnp.float32),
            pltpu.VMEM(row_parts.shape[1:], jnp.float32),
            pltpu.SemaphoreType.DMA((STAGES,)),
        ],
        compiler_params=pltpu.CompilerParams(vmem_limit_bytes=12 * 1024 * 1024),
    )(got, row_parts, col_parts)


def direct_body(covariance, factor_left, factor_right):
    got, row_parts, col_parts, _ = exchange(covariance, factor_left, factor_right)
    held = [pltpu.with_memory_space_constraint(x, pltpu.VMEM) for x in (got, row_parts, col_parts)]
    return scaled(covariance.shape[1], *held)


def power_of_two(n):
    return n & (n - 1) == 0


def chosen(mesh, covariance):
    grid_rows, grid_cols = mesh.shape["prow"], mesh.shape["pcol"]
    tiles = covariance.shape[0] // (grid_rows * grid_cols * TILE)
    fits = tiles == 2 * grid_rows and grid_cols == 8
    across = covariance.shape[1] // (TILE * grid_cols)
    fits = fits and power_of_two(grid_rows) and grid_rows > 1 and across % 4 == 0
    return direct_body if fits else body


def solution(mesh):
    placed = (P(("prow", "pcol"), None), P(None, ("prow", "pcol")), P("prow", "pcol"))

    def run(covariance, factor_left, factor_right):
        return jax.shard_map(
            chosen(mesh, covariance), mesh=mesh, in_specs=placed, out_specs=P("prow", "pcol"), check_vma=False
        )(covariance, factor_left, factor_right)

    return run
```

time: 871 us -> 802 us (0.921)
  blocking collectives: 38.5 us -> 0 us
  matrix products: 28.8 us -> 0 us
  other arithmetic: 27.1 us -> 0 us
  local copies, waits for them, and re-layouts: 4.9 us -> 22.2 us
    psum x2 -> x0, blocking collectives: 38.5 us -> none  [the longest x1 28.4 us: direct_body(): row_total = lax.psum(jnp.sum(squared, axis=1), 'pcol')]
    dot_general x1 -> x0, matrix products: 28.8 us -> none  [direct_body(): jnp.dot(left_rows, right_panel, precision=lax.Precision.HIGH, preferred_e...]
    mul x1 -> x0, other arithmetic: 27.1 us -> none  [direct_body(): corrected * lax.rsqrt(jnp.sqrt(row_mean[:, None] * col_mean[None, :]))]
    pallas_call x1, Pallas kernels: 741 us -> 768 us  [exchange(): pl.pallas_call(functools.partial(exchange_kernel, grid_rows, grid_cols),...]
    unnamed x0 -> x4, local copies, waits for them, and re-layouts: none -> 22.2 us
    pallas_call x1, Pallas kernels: 30.4 us -> 11.1 us  [scaled(): pl.pallas_call(functools.partial(scale_kernel, order), out_shape=jax.Shap...]
where the time goes in v1:
time: 802 us; the launch traced here: 801 us
  Pallas kernels  779 us (97%)
  local copies, waits for them, and re-layouts  22.2 us (3%)
    pallas_call x1, Pallas kernels, exchange(): pl.pallas_call(functools.partial(exchange_kernel, grid_rows, grid_cols),...  768 us
    unnamed x4, local copies, waits for them, and re-layouts  22.2 us

profile of v1, /device:TPU:0, one launch (start us, length us, event | category | flops | bytes accessed | tf_op | source)
XLA Modules:
  0.0 801.3 jit_solution(16359317532026084880)
XLA Ops:
  0.0 768.0 %shard_map.37 = (f32[4096,2048]{1,0:T(8,128)S(1)}, f32[8,32,128]{2,1,0:T(8,128)S(1)}, f32[4,1,2048]{2,1,0:T(1,128)S(1)}, f32[4,8,128,2048]{3,2,1,0:T(8,128)}) custom-call(f32[512,16384]{1,0:T(8,128)} %cov.1, f32[64,512]{1,0:T(8,128)} %left.1, f32[16,2048]{1,0:T(8,128)} %right.1), custom_call_target="tpu_custom_call" | custom-call | tf_op jit(solution)/shard_map/pallas_call | solution.py:354
  768.0 0.0 copy-start
  768.0 11.7 %copy-done = f32[4096,2048]{1,0:T(8,128)} copy-done((f32[4096,2048]{1,0:T(8,128)}, f32[4096,2048]{1,0:T(8,128)S(1)}, u32[]{:S(2)}) %copy-start) | copy-done | bytes 33554456
  779.7 0.0 copy-start.1
  779.7 10.5 %copy-done.1 = f32[4096,2048]{1,0:T(8,128)S(1)} copy-done((f32[4096,2048]{1,0:T(8,128)S(1)}, f32[4096,2048]{1,0:T(8,128)}, u32[]{:S(2)}) %copy-start.1) | copy-done | bytes 33554456
  790.2 11.1 %shard_map.38 = f32[4096,2048]{1,0:T(8,128)} custom-call(f32[4096,2048]{1,0:T(8,128)S(1)} %copy-done.1, f32[8,32,128]{2,1,0:T(8,128)S(1)} %get-tuple-element.9.row_parts, f32[4,1,2048]{2,1,0:T(1,128)S(1)} %get-tuple-element.10.col_parts), custom_call_target="tpu_custom_call" | custom-call | tf_op jit(solution)/shard_map/pallas_call | solution.py:419
Async XLA Ops:
  768.0 11.7 %copy-start = (f32[4096,2048]{1,0:T(8,128)}, f32[4096,2048]{1,0:T(8,128)S(1)}, u32[]{:S(2)}) copy-start(f32[4096,2048]{1,0:T(8,128)S(1)} %get-tuple-element.8.got) | copy-start | bytes 100663296
  779.7 10.5 %copy-start.1 = (f32[4096,2048]{1,0:T(8,128)S(1)}, f32[4096,2048]{1,0:T(8,128)}, u32[]{:S(2)}) copy-start(f32[4096,2048]{1,0:T(8,128)} %copy-done) | copy-start | bytes 100663296

commit v2 on v1

--- a/solution.py
+++ b/solution.py
@@ -65,6 +65,7 @@
 LANES = 128
 CHUNK = 256
 STAGES = 4
+HELD = 26
 
 
 def deal_slab(grid_cols, src, dst):
@@ -119,12 +120,15 @@
         at = ((t % 2) * grid_rows + flip(p, grid_rows, t // 2)) * TILE + h * SLAB
         return pltpu.make_async_copy(cov.at[pl.ds(pl.multiple_of(at, SLAB), SLAB)], slab_in.at[h], in_sem.at[h])
 
+    def slab_slot(t):
+        return jnp.where(t == 0, 2, t % 2)
+
     def slab_store(t, h):
         at = (t % 2) * TILE + h * SLAB
         return pltpu.make_async_copy(
-            slab_out.at[t % 2, h],
+            slab_out.at[slab_slot(t), h],
             tiles.at[flip(p, grid_rows, t // 2), :, pl.ds(pl.multiple_of(at, SLAB), SLAB)],
-            out_sem.at[t % 2, h],
+            out_sem.at[slab_slot(t), h],
         )
 
     for h in range(2):
@@ -172,23 +176,36 @@
             got.at[pl.ds(pl.multiple_of(at, TILE), TILE)], tile_send.at[n], tile_recv.at[n], to,
         )
 
-    def send_tiles(t, kind):
-        dp, k = t // 2, t % 2
+    def send_slab(h):
+        at = pl.multiple_of((p * grid_cols + q) * height + h * SLAB, SLAB)
+        for i in range(2):
+            dz = beside * (3 - i) + (1 - beside) * (1 - i)
+            for dc in range(2):
+                to = target(0, dz, dc)
+                n = (dz * 2 + dc) * 2
+
+                @pl.when(dz + dc != 0)
+                def _():
+                    copy(
+                        slab_out.at[2, h, to[1]], got.at[pl.ds(at, SLAB)], tile_send.at[n], tile_recv.at[n], to
+                    ).start()
+
+    def send_tiles(dp, kind, halves):
         for i in range(2):
             dz = kind * (3 - i) + (1 - kind) * (1 - i)
             for dc in range(2):
-                mine = (dp + dz + dc) == 0
-
-                @pl.when(jnp.logical_not(mine))
+
+                @pl.when(dp + dz + dc != 0)
                 def _():
-                    tile(dp, dz, dc, k).start()
+                    for k in halves:
+                        tile(dp, dz, dc, k).start()
 
     def deal(t, carry):
         @pl.when(t < 2 * grid_rows)
         def _():
             for h in range(2):
                 slab_load(t, h).wait()
-                deal_slab(grid_cols, slab_in.at[h], slab_out.at[t % 2, h])
+                deal_slab(grid_cols, slab_in.at[h], slab_out.at[slab_slot(t), h])
 
                 @pl.when(t + 1 < 2 * grid_rows)
                 def _():
@@ -199,6 +216,7 @@
                 @pl.when((t == 0) & (h == 0))
                 def _():
                     pl.semaphore_wait(barrier, grid_rows * grid_cols - 1)
+                    send_slab(0)
                     keep_left.start()
                     for dp in range(1, grid_rows):
                         plane(dp).start()
@@ -206,6 +224,19 @@
                     for dp in range(1, grid_rows):
                         beside_right(dp).start()
 
+                @pl.when((t == 0) & (h == 1))
+                def _():
+                    send_slab(1)
+
+        @pl.when(t > 0)
+        def _():
+            for h in range(2):
+                slab_store(t - 1, h).wait()
+
+        @pl.when(t == 2)
+        def _():
+            send_tiles(0, beside, (1,))
+
         @pl.when(t == 0)
         def _():
             keep_left.wait()
@@ -214,12 +245,10 @@
             to_gate.start()
             to_mate.start()
 
-        @pl.when(t != 1)
-        def _():
-            s = jnp.maximum(t - 1, 0)
-            for h in range(2):
-                slab_store(s, h).wait()
-            send_tiles(s, beside)
+        @pl.when((t > 2) & (t % 2 == 0))
+        def _():
+            send_tiles(t // 2 - 1, beside, (0, 1))
+            send_tiles(t // 2 - 2, 1 - beside, (0, 1))
 
         return carry
 
@@ -241,12 +270,7 @@
             arrived(2 * (1 - half) + i).wait_recv()
         relay.start()
 
-    def send_rest(t, carry):
-        send_tiles(t, 1 - beside)
-        return carry
-
-    lax.fori_loop(0, 2 * grid_rows, send_rest, 0)
-
+    send_tiles(grid_rows - 1, 1 - beside, (0, 1))
     keep_right.wait()
     for dp in range(1, grid_rows):
         beside_right(dp).wait()
@@ -277,7 +301,7 @@
 
     def settle(m, carry):
         group = m // (2 * grid_rows)
-        dz = jnp.where(group == 3, far, jnp.where(group == 2, 5 - far, group))
+        dz = jnp.where(group == 3, 5 - far, jnp.where(group == 2, far, group))
         dp, dc = m % (2 * grid_rows) // 2, m % 2
         from_p, from_q = target(dp, dz, dc)
         slot = from_p * grid_cols + from_q
@@ -363,19 +387,19 @@
         out_specs=(vmem, vmem, vmem, hbm),
         scratch_shapes=[
             pltpu.VMEM((2, SLAB, breadth), jnp.float32),
-            pltpu.VMEM((2, 2, grid_cols, SLAB, width), jnp.float32),
+            pltpu.VMEM((3, 2, grid_cols, SLAB, width), jnp.float32),
             pltpu.VMEM((grid_rows, rank, height), jnp.float32),
             pltpu.VMEM((2, grid_cols // 2, grid_rows, rank, height), jnp.float32),
             pltpu.VMEM((grid_rows,) + right.shape, jnp.float32),
             pltpu.VMEM((4 * rank, width), jnp.bfloat16),
             pltpu.VMEM((8, width), jnp.float32),
-            dma((2,)), dma((2, 2)), dma((2 * everyone,)), dma((2 * everyone,)),
+            dma((2,)), dma((3, 2)), dma((2 * everyone,)), dma((2 * everyone,)),
             dma((grid_rows,)), dma((grid_rows,)), dma((2,)), dma((grid_cols // 2,)),
             dma, dma, dma, dma, dma((grid_rows,)), dma((grid_rows,)), dma((3,)),
             dma((grid_cols,)), dma((grid_cols,)), dma((grid_rows,)), dma((grid_rows,)),
         ],
         compiler_params=pltpu.CompilerParams(
-            collective_id=0, has_side_effects=True, vmem_limit_bytes=22 * 1024 * 1024
+            collective_id=0, has_side_effects=True, vmem_limit_bytes=HELD * 1024 * 1024
         ),
     )(covariance, left, right)
 
@@ -426,7 +450,7 @@
             pltpu.VMEM(row_parts.shape[1:], jnp.float32),
             pltpu.SemaphoreType.DMA((STAGES,)),
         ],
-        compiler_params=pltpu.CompilerParams(vmem_limit_bytes=12 * 1024 * 1024),
+        compiler_params=pltpu.CompilerParams(vmem_limit_bytes=HELD * 1024 * 1024),
     )(got, row_parts, col_parts)
 
 

time: 802 us -> 752 us (0.938)
  Pallas kernels: 779 us -> 752 us
  local copies, waits for them, and re-layouts: 22.2 us -> 0 us
    pallas_call x1, Pallas kernels: 768 us -> 741 us  [exchange(): pl.pallas_call(functools.partial(exchange_kernel, grid_rows, grid_cols),...]
    unnamed x4 -> x0, local copies, waits for them, and re-layouts: 22.2 us -> none
where the time goes in v2:
time: 752 us
  Pallas kernels  752 us (100%)
    pallas_call x1, Pallas kernels, exchange(): pl.pallas_call(functools.partial(exchange_kernel, grid_rows, grid_cols),...  741 us

profile of v2, /device:TPU:0, one launch (start us, length us, event | category | flops | bytes accessed | tf_op | source)
XLA Modules:
  0.0 752.0 jit_solution(11747893120711574646)
XLA Ops:
  0.0 740.9 %shard_map.37 = (f32[4096,2048]{1,0:T(8,128)S(1)}, f32[8,32,128]{2,1,0:T(8,128)S(1)}, f32[4,1,2048]{2,1,0:T(1,128)S(1)}, f32[4,8,128,2048]{3,2,1,0:T(8,128)}) custom-call(f32[512,16384]{1,0:T(8,128)} %cov.1, f32[64,512]{1,0:T(8,128)} %left.1, f32[16,2048]{1,0:T(8,128)} %right.1), custom_call_target="tpu_custom_call" | custom-call | tf_op jit(solution)/shard_map/pallas_call | solution.py:378
  740.9 11.1 %shard_map.38 = f32[4096,2048]{1,0:T(8,128)} custom-call(f32[4096,2048]{1,0:T(8,128)S(1)} %get-tuple-element.8.got, f32[8,32,128]{2,1,0:T(8,128)S(1)} %get-tuple-element.9.row_parts, f32[4,1,2048]{2,1,0:T(1,128)S(1)} %get-tuple-element.10.col_parts), custom_call_target="tpu_custom_call" | custom-call | tf_op jit(solution)/shard_map/pallas_call | solution.py:443

commit v3 on v2

--- a/solution.py
+++ b/solution.py
@@ -83,7 +83,7 @@
 def exchange_kernel(
     grid_rows, grid_cols,
     cov, left, right, got, row_parts, col_parts, tiles,
-    slab_in, slab_out, left_own, lefts, rights, right_split, col_sum,
+    slab_in, slab_out, left_in, left_own, lefts, rights, right_split, col_sum,
     in_sem, out_sem, tile_send, tile_recv, plane_send, plane_recv, block_send, block_recv,
     relay_send, relay_recv, swap_send, swap_recv, right_send, right_recv, own_sem,
     row_send, row_recv, col_send, col_recv,
@@ -107,6 +107,26 @@
     def target(dp, dz, dc):
         return flip(p, grid_rows, dp), 2 * flip(z, chips, dz) + (core + dc) % 2
 
+    def slab_load(t, h):
+        at = ((t % 2) * grid_rows + flip(p, grid_rows, t // 2)) * TILE + h * SLAB
+        return pltpu.make_async_copy(cov.at[pl.ds(pl.multiple_of(at, SLAB), SLAB)], slab_in.at[h], in_sem.at[h])
+
+    def slab_slot(t):
+        return jnp.where(t == 0, 2, t % 2)
+
+    def slab_store(t, h):
+        at = (t % 2) * TILE + h * SLAB
+        return pltpu.make_async_copy(
+            slab_out.at[slab_slot(t), h],
+            tiles.at[flip(p, grid_rows, t // 2), :, pl.ds(pl.multiple_of(at, SLAB), SLAB)],
+            out_sem.at[slab_slot(t), h],
+        )
+
+    for h in range(2):
+        slab_load(0, h).start()
+    load_left = pltpu.make_async_copy(left, left_in, own_sem.at[3])
+    load_left.start()
+
     barrier = pltpu.get_barrier_semaphore()
     for dp in range(grid_rows):
         for dz in range(chips):
@@ -116,34 +136,17 @@
                         barrier, inc=1, device_id=target(dp, dz, dc), device_id_type=pl.DeviceIdType.MESH
                     )
 
-    def slab_load(t, h):
-        at = ((t % 2) * grid_rows + flip(p, grid_rows, t // 2)) * TILE + h * SLAB
-        return pltpu.make_async_copy(cov.at[pl.ds(pl.multiple_of(at, SLAB), SLAB)], slab_in.at[h], in_sem.at[h])
-
-    def slab_slot(t):
-        return jnp.where(t == 0, 2, t % 2)
-
-    def slab_store(t, h):
-        at = (t % 2) * TILE + h * SLAB
-        return pltpu.make_async_copy(
-            slab_out.at[slab_slot(t), h],
-            tiles.at[flip(p, grid_rows, t // 2), :, pl.ds(pl.multiple_of(at, SLAB), SLAB)],
-            out_sem.at[slab_slot(t), h],
-        )
-
-    for h in range(2):
-        slab_load(0, h).start()
-
-    low = lax.broadcasted_iota(jnp.int32, (rank, LANES), 1) < TILE
-    for to in range(grid_rows):
-        at = to // 2 * LANES
-        first = left[:, at:at + LANES]
-        at += grid_rows * TILE
-        second = left[:, at:at + LANES]
-        if to % 2 == 0:
-            left_own[to] = jnp.where(low, first, pltpu.roll(second, TILE, 1))
-        else:
-            left_own[to] = jnp.where(low, pltpu.roll(first, TILE, 1), second)
+    def pick_left():
+        low = lax.broadcasted_iota(jnp.int32, (rank, LANES), 1) < TILE
+        for to in range(grid_rows):
+            at = to // 2 * LANES
+            first = left_in[:, at:at + LANES]
+            at += grid_rows * TILE
+            second = left_in[:, at:at + LANES]
+            if to % 2 == 0:
+                left_own[to] = jnp.where(low, first, pltpu.roll(second, TILE, 1))
+            else:
+                left_own[to] = jnp.where(low, pltpu.roll(first, TILE, 1), second)
 
     def plane(dp):
         return copy(
@@ -167,13 +170,12 @@
     own_rows = pl.ds(pl.multiple_of((p * grid_cols + q) * height, height), height)
     keep_tiles = pltpu.make_async_copy(tiles.at[p, q], got.at[own_rows], own_sem.at[2])
 
-    def tile(dp, dz, dc, k):
+    def tile(dp, dz, dc, start, count):
         to = target(dp, dz, dc)
-        at = (p * grid_cols + q) * height + k * TILE
-        n = ((dp * chips + dz) * 2 + dc) * 2 + k
+        at = pl.multiple_of((p * grid_cols + q) * height + start, TILE)
+        n = (dp * chips + dz) * 2 + dc
         return copy(
-            tiles.at[to[0], to[1], pl.ds(pl.multiple_of(k * TILE, TILE), TILE)],
-            got.at[pl.ds(pl.multiple_of(at, TILE), TILE)], tile_send.at[n], tile_recv.at[n], to,
+            tiles.at[to[0], to[1], pl.ds(start, count)], got.at[pl.ds(at, count)], tile_send.at[n], tile_recv.at[n], to
         )
 
     def send_slab(h):
@@ -182,7 +184,7 @@
             dz = beside * (3 - i) + (1 - beside) * (1 - i)
             for dc in range(2):
                 to = target(0, dz, dc)
-                n = (dz * 2 + dc) * 2
+                n = dz * 2 + dc
 
                 @pl.when(dz + dc != 0)
                 def _():
@@ -190,15 +192,14 @@
                         slab_out.at[2, h, to[1]], got.at[pl.ds(at, SLAB)], tile_send.at[n], tile_recv.at[n], to
                     ).start()
 
-    def send_tiles(dp, kind, halves):
+    def send_tiles(dp, kind, start=0):
         for i in range(2):
             dz = kind * (3 - i) + (1 - kind) * (1 - i)
             for dc in range(2):
 
                 @pl.when(dp + dz + dc != 0)
                 def _():
-                    for k in halves:
-                        tile(dp, dz, dc, k).start()
+                    tile(dp, dz, dc, start, height - start).start()
 
     def deal(t, carry):
         @pl.when(t < 2 * grid_rows)
@@ -217,16 +218,18 @@
                 def _():
                     pl.semaphore_wait(barrier, grid_rows * grid_cols - 1)
                     send_slab(0)
+                    load_left.wait()
+                    pick_left()
+                    keep_right.start()
+                    for dp in range(1, grid_rows):
+                        beside_right(dp).start()
+
+                @pl.when((t == 0) & (h == 1))
+                def _():
+                    send_slab(1)
                     keep_left.start()
                     for dp in range(1, grid_rows):
                         plane(dp).start()
-                    keep_right.start()
-                    for dp in range(1, grid_rows):
-                        beside_right(dp).start()
-
-                @pl.when((t == 0) & (h == 1))
-                def _():
-                    send_slab(1)
 
         @pl.when(t > 0)
         def _():
@@ -235,9 +238,9 @@
 
         @pl.when(t == 2)
         def _():
-            send_tiles(0, beside, (1,))
-
-        @pl.when(t == 0)
+            send_tiles(0, beside, TILE)
+
+        @pl.when(t == 1)
         def _():
             keep_left.wait()
             for dp in range(1, grid_rows):
@@ -247,8 +250,8 @@
 
         @pl.when((t > 2) & (t % 2 == 0))
         def _():
-            send_tiles(t // 2 - 1, beside, (0, 1))
-            send_tiles(t // 2 - 2, 1 - beside, (0, 1))
+            send_tiles(t // 2 - 1, beside)
+            send_tiles(t // 2 - 2, 1 - beside)
 
         return carry
 
@@ -270,7 +273,7 @@
             arrived(2 * (1 - half) + i).wait_recv()
         relay.start()
 
-    send_tiles(grid_rows - 1, 1 - beside, (0, 1))
+    send_tiles(grid_rows - 1, 1 - beside)
     keep_right.wait()
     for dp in range(1, grid_rows):
         beside_right(dp).wait()
@@ -308,12 +311,9 @@
 
         @pl.when(dp + dz + dc != 0)
         def _():
-            for k in range(2):
-                n = ((dp * chips + dz) * 2 + dc) * 2 + k
-                there = got.at[pl.ds(pl.multiple_of(slot * height + k * TILE, TILE), TILE)]
-                copy(
-                    tiles.at[0, 0, pl.ds(0, TILE)], there, tile_send.at[n], tile_recv.at[n], (from_p, from_q)
-                ).wait_recv()
+            n = (dp * chips + dz) * 2 + dc
+            there = got.at[pl.ds(pl.multiple_of(slot * height, height), height)]
+            copy(tiles.at[0, 0], there, tile_send.at[n], tile_recv.at[n], (from_p, from_q)).wait_recv()
 
         value = lefts[from_q % 2, from_q // 2, from_p]
         high = value.astype(jnp.bfloat16).astype(jnp.float32)
@@ -353,13 +353,10 @@
         col_part(dp).start()
 
     def drain(n, carry):
-        @pl.when(n > 1)
-        def _():
-            tile(n // (4 * chips), n // 4 % chips, n // 2 % 2, n % 2).wait_send()
-
+        tile(n // (2 * chips), n // 2 % chips, n % 2, 0, height).wait_send()
         return carry
 
-    lax.fori_loop(0, 2 * grid_rows * grid_cols, drain, 0)
+    lax.fori_loop(1, grid_rows * grid_cols, drain, 0)
     for n in range(1, grid_cols):
         row_part(n).wait()
     for dp in range(1, grid_rows):
@@ -383,19 +380,20 @@
             pltpu.VMEM((grid_rows, 1, width), jnp.float32),
             pltpu.HBM((grid_rows, grid_cols, height, width), jnp.float32),
         ),
-        in_specs=[hbm, vmem, vmem],
+        in_specs=[hbm] * 3,
         out_specs=(vmem, vmem, vmem, hbm),
         scratch_shapes=[
             pltpu.VMEM((2, SLAB, breadth), jnp.float32),
             pltpu.VMEM((3, 2, grid_cols, SLAB, width), jnp.float32),
+            pltpu.VMEM(left.shape, jnp.float32),
             pltpu.VMEM((grid_rows, rank, height), jnp.float32),
             pltpu.VMEM((2, grid_cols // 2, grid_rows, rank, height), jnp.float32),
             pltpu.VMEM((grid_rows,) + right.shape, jnp.float32),
             pltpu.VMEM((4 * rank, width), jnp.bfloat16),
             pltpu.VMEM((8, width), jnp.float32),
-            dma((2,)), dma((3, 2)), dma((2 * everyone,)), dma((2 * everyone,)),
+            dma((2,)), dma((3, 2)), dma((everyone,)), dma((everyone,)),
             dma((grid_rows,)), dma((grid_rows,)), dma((2,)), dma((grid_cols // 2,)),
-            dma, dma, dma, dma, dma((grid_rows,)), dma((grid_rows,)), dma((3,)),
+            dma, dma, dma, dma, dma((grid_rows,)), dma((grid_rows,)), dma((4,)),
             dma((grid_cols,)), dma((grid_cols,)), dma((grid_rows,)), dma((grid_rows,)),
         ],
         compiler_params=pltpu.CompilerParams(

time: 752 us -> 751 us (level)
  no operation moved by 1% of the time
where the time goes in v3:
time: 751 us
  Pallas kernels  751 us (100%)
    pallas_call x1, Pallas kernels, exchange(): pl.pallas_call(functools.partial(exchange_kernel, grid_rows, grid_cols),...  739 us

profile of v3, /device:TPU:0, one launch (start us, length us, event | category | flops | bytes accessed | tf_op | source)
XLA Modules:
  0.0 750.6 jit_solution(9391372736243313979)
XLA Ops:
  0.0 739.5 %shard_map.37 = (f32[4096,2048]{1,0:T(8,128)S(1)}, f32[8,32,128]{2,1,0:T(8,128)S(1)}, f32[4,1,2048]{2,1,0:T(1,128)S(1)}, f32[4,8,128,2048]{3,2,1,0:T(8,128)}) custom-call(f32[512,16384]{1,0:T(8,128)} %cov.1, f32[64,512]{1,0:T(8,128)} %left.1, f32[16,2048]{1,0:T(8,128)} %right.1), custom_call_target="tpu_custom_call" | custom-call | tf_op jit(solution)/shard_map/pallas_call | solution.py:375
  739.5 11.1 %shard_map.38 = f32[4096,2048]{1,0:T(8,128)} custom-call(f32[4096,2048]{1,0:T(8,128)S(1)} %get-tuple-element.8.got, f32[8,32,128]{2,1,0:T(8,128)S(1)} %get-tuple-element.9.row_parts, f32[4,1,2048]{2,1,0:T(1,128)S(1)} %get-tuple-element.10.col_parts), custom_call_target="tpu_custom_call" | custom-call | tf_op jit(solution)/shard_map/pallas_call | solution.py:441

commit v4 on v3

--- a/solution.py
+++ b/solution.py
@@ -285,7 +285,7 @@
         right_split[n * depth:(n + 1) * depth] = high
         right_split[rank + n * depth:rank + (n + 1) * depth] = rest
         right_split[2 * rank + n * depth:2 * rank + (n + 1) * depth] = high
-        right_split[3 * rank + n * depth:3 * rank + (n + 1) * depth] = jnp.zeros_like(high)
+        right_split[3 * rank + n * depth:3 * rank + (n + 1) * depth] = rest
     col_sum[...] = jnp.zeros_like(col_sum)
 
     @pl.when(beside == 0)
@@ -317,7 +317,7 @@
 
         value = lefts[from_q % 2, from_q // 2, from_p]
         high = value.astype(jnp.bfloat16).astype(jnp.float32)
-        stack = jnp.concatenate([high, high, value - high, jnp.zeros_like(high)], axis=0)
+        stack = jnp.concatenate([high, high, value - high, value - high], axis=0)
         factor = stack.T.astype(jnp.bfloat16)
         rows = pl.ds(pl.multiple_of(slot * height, height), height)
         total = jnp.zeros((height, LANES), jnp.float32)

time: 751 us -> 751 us (level)
  no operation moved by 1% of the time
where the time goes in v4:
time: 751 us
  Pallas kernels  751 us (100%)
    pallas_call x1, Pallas kernels, exchange(): pl.pallas_call(functools.partial(exchange_kernel, grid_rows, grid_cols),...  739 us

profile of v4, /device:TPU:0, one launch (start us, length us, event | category | flops | bytes accessed | tf_op | source)
XLA Modules:
  0.0 750.6 jit_solution(15420280839120492718)
XLA Ops:
  0.0 739.5 %shard_map.37 = (f32[4096,2048]{1,0:T(8,128)S(1)}, f32[8,32,128]{2,1,0:T(8,128)S(1)}, f32[4,1,2048]{2,1,0:T(1,128)S(1)}, f32[4,8,128,2048]{3,2,1,0:T(8,128)}) custom-call(f32[512,16384]{1,0:T(8,128)} %cov.1, f32[64,512]{1,0:T(8,128)} %left.1, f32[16,2048]{1,0:T(8,128)} %right.1), custom_call_target="tpu_custom_call" | custom-call | tf_op jit(solution)/shard_map/pallas_call | solution.py:375
  739.5 11.1 %shard_map.38 = f32[4096,2048]{1,0:T(8,128)} custom-call(f32[4096,2048]{1,0:T(8,128)S(1)} %get-tuple-element.8.got, f32[8,32,128]{2,1,0:T(8,128)S(1)} %get-tuple-element.9.row_parts, f32[4,1,2048]{2,1,0:T(1,128)S(1)} %get-tuple-element.10.col_parts), custom_call_target="tpu_custom_call" | custom-call | tf_op jit(solution)/shard_map/pallas_call | solution.py:441
